TPU v7x, 32 devices: a 4x4x1 block of a 4x4x8 slice. The times are simulated.
32 devices in a mesh: dp: 1 (over z), tp: 4 (over y), ep: 8 (over x, core).
Axes of the slice: x: 4, y: 4, z: 1, core: 2. Of those that a mesh axis runs over, the one named last changes fastest.
The devices are a block of a 4x4x8 slice.
Arguments:
- tokens: bfloat16 [8192, 768], P(('dp', 'ep', 'tp'))
- expert_ids: int32 [8192, 2], P(('dp', 'ep', 'tp'))
- gate_vals: float32 [8192, 2], P(('dp', 'ep', 'tp'))
- w_up: bfloat16 [64, 768, 3072], P('ep', None, 'tp')
- w_down: bfloat16 [64, 3072, 768], P('ep', 'tp')
Outputs:
- output: bfloat16 [8192, 768], P(('dp', 'ep', 'tp'))
All inputs are finite; a program needn't handle non-finite values.
Results may differ from a plain program's by a relative error of at most 0.001.
Values are sent between devices in bfloat16 or wider.
A program may use at most 768 MiB of HBM per device.

v0:
```python
import jax
import jax.numpy as jnp
from jax import lax
from jax.sharding import PartitionSpec as P


def capacity(tok_count, n_top, n_exp):
    return ((5 * tok_count * n_top) // (4 * n_exp) + 7) // 8 * 8


def slot_table(route_ids, n_exp, slot_cap):
    expert_hit = (route_ids[:, :, None] == jnp.arange(n_exp, dtype=jnp.int32)).astype(jnp.int32)
    chosen = jnp.sum(expert_hit, axis=1)
    prior_count = jnp.cumsum(chosen, axis=0) - chosen
    token_rank = jnp.sum(expert_hit * prior_count[:, None, :], axis=2)
    return jnp.where(token_rank < slot_cap, route_ids * slot_cap + token_rank, -1)


def solution(mesh):
    n_ep = mesh.shape['ep']
    row_spec = P(('dp', 'ep', 'tp'), None)

    def local_moe(tokens, expert_ids, gate_vals, w_up, w_down):
        tok_count, hidden = tokens.shape
        n_top = expert_ids.shape[1]
        local_exp = w_up.shape[0]
        n_exp = local_exp * n_ep
        slot_cap = capacity(tok_count, n_top, n_exp)
        n_slots = n_exp * slot_cap
        slot_ids = slot_table(expert_ids, n_exp, slot_cap)
        slot_iota = jnp.arange(n_slots, dtype=jnp.int32)
        pick_mat = jnp.zeros((n_slots, tok_count), jnp.bfloat16)
        for choice_idx in range(n_top):
            pick_mat = pick_mat + (slot_iota[:, None] == slot_ids[None, :, choice_idx]).astype(jnp.bfloat16)
        send_buf = jnp.dot(pick_mat, tokens, preferred_element_type=jnp.float32).astype(jnp.bfloat16)
        send_buf = send_buf.reshape(n_exp, slot_cap, hidden)
        arrived = lax.all_to_all(send_buf, 'ep', 0, 1, tiled=True)
        gathered = lax.all_gather(arrived, 'tp', axis=1, tiled=True)
        pre_act = jnp.einsum('ech,ehf->ecf', gathered, w_up, preferred_element_type=jnp.float32)
        hidden_act = jax.nn.gelu(pre_act, approximate=True).astype(jnp.bfloat16)
        part_out = jnp.einsum('ecf,efh->ech', hidden_act, w_down, preferred_element_type=jnp.float32)
        reduced = lax.psum_scatter(part_out, 'tp', scatter_dimension=1, tiled=True).astype(jnp.bfloat16)
        returned = lax.all_to_all(reduced, 'ep', 1, 0, tiled=True).reshape(n_slots, hidden)
        gate_sum = jnp.zeros((tok_count, hidden), jnp.float32)
        for choice_idx in range(n_top):
            pick_row = (slot_ids[:, choice_idx, None] == slot_iota[None, :]).astype(jnp.bfloat16)
            picked = jnp.dot(pick_row, returned, preferred_element_type=jnp.float32)
            gate_sum = gate_sum + gate_vals[:, choice_idx, None] * picked
        return gate_sum.astype(jnp.bfloat16)

    return jax.shard_map(local_moe, mesh=mesh,
                         in_specs=(row_spec, row_spec, row_spec, P('ep', None, 'tp'), P('ep', 'tp', None)),
                         out_specs=row_spec, check_vma=False)
```

profile of v0, /device:TPU:97, one launch (start us, length us, event | category | flops | bytes accessed | tf_op | source)
XLA Modules:
  0.0 271.9 jit_solution(9955856195575855206)
XLA Ops:
  6.5 0.0 copy-start
  6.6 0.0 all-gather.2.cloned.1.call-start
  6.6 0.8 convert_reduce_fusion
  7.3 0.6 reduce-window.6
  7.9 0.2 slice_reduce_fusion
  8.2 0.1 fusion.25
  8.3 0.7 select_reduce_fusion
  9.0 0.7 compare_select_fusion
  9.7 0.6 convolution_convert_fusion
  10.3 26.4 %all_to_all.33 = bf16[64,16,768]{2,1,0:T(8,128)(2,1)S(1)} all-to-all(bf16[64,16,768]{2,1,0:T(8,128)(2,1)S(1)} %bitcast.49), channel_id=1, replica_groups=mesh['dp'=1,'tp'=4,'ep'=8] {'ep'}, dimensions={0} | all-to-all | bytes 3145728 | tf_op jit(solution)/shard_map/all_to_all | solution.py:37
  36.7 1.3 copy.30
  38.0 0.1 all-gather.2.cloned.1.call-update
  38.0 0.1 reduce-scatter.2.cloned.1.call-start
  38.1 64.5 %all-gather.2.cloned.1.call-done = bf16[8,512,768]{2,1,0:T(8,128)(2,1)} async-done(((bf16[8,128,768]{2,1,0:T(8,128)(2,1)}), bf16[8,512,768]{2,1,0:T(8,128)(2,1)}) %all-gather.2.cloned.1.call-update) | async-done | bytes 6291472 | tf_op jit(solution)/shard_map/all_gather | solution.py:38
  102.6 17.5 %fusion.8 = f32[8,512,768]{2,1,0:T(8,128)} fusion(bf16[8,768,768]{2,1,0:T(8,128)(2,1)} %param.9, bf16[8,512,768]{2,1,0:T(8,128)(2,1)} %all-gather.2.cloned.1.call-done, bf16[8,768,768]{2,1,0:T(8,128)(2,1)} %param.8), kind=kOutput, calls=%fused_computation.9 | convolution fusion | flops 9691987968 | bytes 37748736 | tf_op jit(solution)/shard_map/ecf,efh->ech/dot_general | solution.py:41
  120.1 0.1 reduce-scatter.2.cloned.1.call-update
  120.2 112.8 %reduce-scatter.2.cloned.1.call-done = f32[8,128,768]{2,1,0:T(8,128)} async-done(((f32[8,512,768]{2,1,0:T(8,128)}), f32[8,128,768]{2,1,0:T(8,128)}) %reduce-scatter.2.cloned.1.call-update) | async-done | bytes 3145744 | tf_op jit(solution)/shard_map/reduce_scatter | solution.py:42
  233.0 2.1 convert_element_type.28
  235.1 2.0 copy.31
  237.1 5.2 %all-to-all-start.1 = ((bf16[8,128,768]{2,0,1:T(8,128)(2,1)}), bf16[8,128,768]{2,0,1:T(8,128)(2,1)S(1)}, u32[]{:S(2)}, u32[]{:S(2)}) async-start(bf16[8,128,768]{2,0,1:T(8,128)(2,1)} %copy.31), calls=%async_computation.2 | async-start | bytes 3145728 | tf_op jit(solution)/shard_map/all_to_all | solution.py:43
  242.3 20.4 %all-to-all-done.1 = bf16[8,128,768]{2,0,1:T(8,128)(2,1)S(1)} async-done(((bf16[8,128,768]{2,0,1:T(8,128)(2,1)}), bf16[8,128,768]{2,0,1:T(8,128)(2,1)S(1)}, u32[]{:S(2)}, u32[]{:S(2)}) %all-to-all-start.1) | async-done | bytes 1572896 | tf_op jit(solution)/shard_map/all_to_all | solution.py:43
  262.6 0.3 copy.33
  263.0 0.6 convolution_multiply_fusion.1
  263.6 1.4 fusion.15
  (8 shorter events, 0.1 us)
Async XLA Ops:
  6.5 3.1 %copy-start = (bf16[256,768]{1,0:T(8,128)(2,1)S(1)}, bf16[256,768]{1,0:T(8,128)(2,1)}, u32[]{:S(2)}) copy-start(bf16[256,768]{1,0:T(8,128)(2,1)} %param.5) | copy-start | bytes 1179652
  6.6 96.1 %all-gather.2.cloned.1.call-start = ((), (), s32[]{:S(2)}) async-start(), calls=%async_computation.3 | async-start | bytes 7864320 | tf_op jit(solution)/shard_map/all_gather | solution.py:38
  38.0 195.0 %reduce-scatter.2.cloned.1.call-start = ((), (), s32[]{:S(2)}) async-start(), calls=%async_computation.4 | async-start | bytes 15728640 | tf_op jit(solution)/shard_map/reduce_scatter | solution.py:42
  120.1 122.2 %copy-start.1 = (f32[256,2]{0,1:T(2,128)S(1)}, f32[256,2]{0,1:T(2,128)}, u32[]{:S(2)}) copy-start(f32[256,2]{0,1:T(2,128)} %param.7) | copy-start | bytes 6148
  237.1 25.6 %all-to-all-start.1 = ((bf16[8,128,768]{2,0,1:T(8,128)(2,1)}), bf16[8,128,768]{2,0,1:T(8,128)(2,1)S(1)}, u32[]{:S(2)}, u32[]{:S(2)}) async-start(bf16[8,128,768]{2,0,1:T(8,128)(2,1)} %copy.31), calls=%async_computation.2 | async-start | bytes 3145728 | tf_op jit(solution)/shard_map/all_to_all | solution.py:43
Sparse Core Ops, SparseCore 0:
  38.1 64.4 all-gather.1
  120.3 112.6 reduce-scatter.1
where the time goes:
time: 272 us
  waiting for transfers between devices  198 us (73%)
  blocking collectives  26.4 us (10%)
  matrix products  20.2 us (7%)
  between operations  13.5 us (5%)
  starting transfers between devices  5.26 us (2%)
  other arithmetic  4.95 us (2%)
  local copies, waits for them, and re-layouts  3.82 us (1%)
    reduce_scatter x1, waiting for transfers between devices, local_moe(): lax.psum_scatter(part_out, 'tp', scatter_dimension=1, tiled=True)  113 us
    all_gather x1, waiting for transfers between devices, local_moe(): gathered = lax.all_gather(arrived, 'tp', axis=1, tiled=True)  64.5 us
    all_to_all x1, blocking collectives, local_moe(): arrived = lax.all_to_all(send_buf, 'ep', 0, 1, tiled=True)  26.4 us
    all_to_all x1, waiting for transfers between devices, local_moe(): lax.all_to_all(reduced, 'ep', 1, 0, tiled=True).reshape(n_slots, hidden)  20.4 us
    dot_general x1, matrix products, local_moe(): jnp.einsum('ecf,efh->ech', hidden_act, w_down, preferred_element_type=jnp...  17.5 us
  transfers between devices with their start and end apart: 3, of which 3 were waited for; matrix products, arithmetic and copies ran while one was open for 0% of the time, Pallas kernels for 0%

commit v1 on v0

v1 whole, which is shorter than its diff:
```python
import functools

import jax
import jax.numpy as jnp
from jax import lax
from jax.experimental import pallas as pl
from jax.experimental.pallas import tpu as pltpu
from jax.sharding import PartitionSpec as P

MESH = pl.DeviceIdType.MESH
ID_ROWS = 16


def capacity(tok_count, n_top, n_exp):
    return ((5 * tok_count * n_top) // (4 * n_exp) + 7) // 8 * 8


def rem(a, b):
    return a % b if isinstance(a, int) else lax.rem(a, b)


def div(a, b):
    return a // b if isinstance(a, int) else lax.div(a, b)


def moe_kernel(n_tp, n_ep, slot_cap, tokens, id_rows, ids_col, gates, w_up, w_down, out,
               tok, up, down, tri, xbuf, part, r1, r2, red, ret, slot_col, acc,
               load_sem, w_sem, full_send, full_recv, half_send, half_recv,
               r1_send, r1_recv, r2_send, r2_recv, ret_send, ret_recv):
    t = lax.axis_index("tp")
    e = lax.axis_index("ep")
    n_chip = n_ep // 2
    x = div(e, 2)
    c = rem(e, 2)
    n_tok, hidden = tokens.shape
    n_loc = w_up.shape[0]
    n_top = ids_col.shape[1]
    n_exp = n_loc * n_ep
    rows = n_tok + ID_ROWS
    half_rows = n_tok // 2
    half_exp = n_loc // 2
    sub_rows = half_exp * slot_cap
    sub_half = sub_rows // 2
    n_sub = 2 * n_ep
    t_up = rem(t + 1, n_tp)
    t_dn = rem(t + n_tp - 1, n_tp)
    t_far = rem(t + 2, n_tp)
    x_up = rem(x + 1, n_chip)
    x_dn = rem(x + n_chip - 1, n_chip)
    x_far = rem(x + 2, n_chip)
    up_ep = x_up * 2 + c
    dn_ep = x_dn * 2 + c
    mate_ep = x * 2 + (1 - c)

    def block(ep, tp):
        return ep * n_tp + tp

    own = block(e, t)
    own_copies = [
        pltpu.make_async_copy(tokens, tok.at[own, pl.ds(0, n_tok)], load_sem.at[0]),
        pltpu.make_async_copy(id_rows, tok.at[own, pl.ds(n_tok, ID_ROWS)], load_sem.at[1]),
    ]
    for copy in own_copies:
        copy.start()
    w_copies = []
    for i in range(n_loc):
        w_copies.append(pltpu.make_async_copy(w_up.at[i], up.at[i], w_sem.at[0, i]))
        w_copies.append(pltpu.make_async_copy(w_down.at[i], down.at[i], w_sem.at[1, i]))
    for copy in w_copies:
        copy.start()

    barrier = pltpu.get_barrier_semaphore()
    for tp in (t_up, t_dn):
        pl.semaphore_signal(barrier, inc=1, device_id={"tp": tp, "ep": e}, device_id_type=MESH)
    for step in range(1, n_ep):
        pl.semaphore_signal(barrier, inc=1, device_id={"tp": t, "ep": rem(e + step, n_ep)}, device_id_type=MESH)

    row_i = lax.broadcasted_iota(jnp.int32, (n_tok, n_tok), 0)
    col_i = lax.broadcasted_iota(jnp.int32, (n_tok, n_tok), 1)
    tri[...] = jnp.where(row_i < col_i, 1.0, 0.0).astype(jnp.bfloat16)
    lower = jnp.where(row_i > col_i, 1.0, 0.0).astype(jnp.bfloat16)
    lanes = max(128, n_exp)
    lane_i = lax.broadcasted_iota(jnp.int32, (n_tok, lanes), 1)
    hit_sum = jnp.zeros((n_tok, lanes), jnp.float32)
    for j in range(n_top):
        hit_sum = hit_sum + jnp.where(ids_col[:, j:j + 1] == lane_i, 1.0, 0.0)
    prior = jnp.dot(lower, hit_sum.astype(jnp.bfloat16), preferred_element_type=jnp.float32)
    for j in range(n_top):
        ids_j = ids_col[:, j:j + 1]
        rank = jnp.sum(jnp.where(ids_j == lane_i, prior, 0.0), axis=1, keepdims=True).astype(jnp.int32)
        slot_col[:, j:j + 1] = jnp.where(rank < slot_cap, ids_j * slot_cap + rank, -1)
    acc[...] = jnp.zeros_like(acc)

    sends = []

    def send(make):
        make().start()
        sends.append(make)

    def remote(src, dst, send_sem, recv_sem, tp, ep):
        return pltpu.make_async_remote_copy(src_ref=src, dst_ref=dst, send_sem=send_sem, recv_sem=recv_sem,
                                            device_id={"tp": tp, "ep": ep}, device_id_type=MESH)

    n_full = [0]
    n_half = [0]

    def send_full(src, tp, ep):
        n = n_full[0]
        n_full[0] += 1

        def make():
            b = block(*src)
            return remote(tok.at[b], tok.at[b], full_send.at[n], full_recv.at[b], tp, ep)
        send(make)

    def half_of(b, which):
        return tok.at[b, pl.ds(0, half_rows)] if which == 0 else tok.at[b, pl.ds(half_rows, rows - half_rows)]

    def send_half(src, which, tp, ep):
        n = n_half[0]
        n_half[0] += 1

        def make():
            b = block(*src)
            ref = half_of(b, which)
            return remote(ref, ref, half_send.at[n], half_recv.at[which, b], tp, ep)
        send(make)

    def wait_full(src):
        b = block(*src)
        pltpu.make_async_copy(tok.at[b], tok.at[b], full_recv.at[b]).wait()

    def wait_half(src, which):
        b = block(*src)
        ref = half_of(b, which)
        pltpu.make_async_copy(ref, ref, half_recv.at[which, b]).wait()

    def spread(src):
        send_full(src, t, up_ep)
        send_full(src, t, dn_ep)
        send_full(src, t, mate_ep)

    for copy in own_copies:
        copy.wait()
    pl.semaphore_wait(barrier, n_ep + 1)
    send_full((e, t), t_up, e)
    send_full((e, t), t_dn, e)
    spread((e, t))
    wait_full((e, t_dn))
    send_half((e, t_dn), 0, t_up, e)
    spread((e, t_dn))
    wait_full((e, t_up))
    send_half((e, t_up), 1, t_dn, e)
    spread((e, t_up))
    wait_half((e, t_far), 0)
    wait_half((e, t_far), 1)
    spread((e, t_far))

    def relay(tp):
        wait_full((dn_ep, tp))
        send_half((dn_ep, tp), 0, t, up_ep)
        send_full((dn_ep, tp), t, mate_ep)
        wait_full((up_ep, tp))
        send_half((up_ep, tp), 1, t, dn_ep)
        send_full((up_ep, tp), t, mate_ep)

    far_ep = x_far * 2 + c

    def far_block(tp):
        wait_half((far_ep, tp), 0)
        wait_half((far_ep, tp), 1)
        send_full((far_ep, tp), t, mate_ep)

    def source_ep(k):
        return rem(x + div(k, 2), n_chip) * 2 + rem(c + k, 2)

    def pick(s):
        exp_i = lax.broadcasted_iota(jnp.int32, (n_loc, n_tok), 0) + e * n_loc
        hits = []
        for tp in range(n_tp):
            row = tok[block(s, tp), n_tok:rows, 0:n_top * n_tok].astype(jnp.float32)
            hit = jnp.zeros((n_loc, n_tok), jnp.float32)
            for j in range(n_top):
                ids = row[0:1, j * n_tok:(j + 1) * n_tok].astype(jnp.int32)
                hit = hit + jnp.where(ids == exp_i, 1.0, 0.0)
            hits.append(hit)
        hit = jnp.concatenate(hits, axis=0)
        prior = jnp.dot(hit.astype(jnp.bfloat16), tri[...], preferred_element_type=jnp.float32)
        rank = jnp.where(hit > 0.0, prior, -1.0)
        slot_i = lax.broadcasted_iota(jnp.int32, (slot_cap, n_tok), 0).astype(jnp.float32)
        for tp in range(n_tp):
            picks = []
            for i in range(n_loc):
                r = tp * n_loc + i
                picks.append(jnp.where(rank[r:r + 1] == slot_i, 1.0, 0.0))
            onehot = jnp.concatenate(picks, axis=0).astype(jnp.bfloat16)
            got = jnp.dot(onehot, tok[block(s, tp), 0:n_tok, :], preferred_element_type=jnp.float32)
            got = got.astype(jnp.bfloat16)
            for i in range(n_loc):
                xbuf[i, tp * slot_cap:(tp + 1) * slot_cap, :] = got[i * slot_cap:(i + 1) * slot_cap]

    def ffn(i):
        h = rem(i, 2)

        def one(q, carry):
            w = h * half_exp + q
            pre = jnp.dot(xbuf[w], up[w], preferred_element_type=jnp.float32)
            act = jax.nn.gelu(pre, approximate=True).astype(jnp.bfloat16)
            res = jnp.dot(act, down[w], preferred_element_type=jnp.float32)
            for tp in range(n_tp):
                part[i, tp, pl.ds(pl.multiple_of(q * slot_cap, slot_cap), slot_cap), :] = (
                    res[tp * slot_cap:(tp + 1) * slot_cap])
            return carry

        lax.fori_loop(0, half_exp, one, 0)

    lo = pl.ds(0, sub_half)
    hi = pl.ds(sub_half, sub_half)

    def r_copy(src, dst, send_sem, recv_sem, tp):
        return pltpu.make_async_remote_copy(src_ref=src, dst_ref=dst, send_sem=send_sem, recv_sem=recv_sem,
                                            device_id={"tp": tp, "ep": e}, device_id_type=MESH)

    def first_copies(i):
        return [
            r_copy(part.at[i, t_far, lo], r1.at[0, i], r1_send.at[0, i], r1_recv.at[0, i], t_up),
            r_copy(part.at[i, t_far, hi], r1.at[1, i], r1_send.at[1, i], r1_recv.at[1, i], t_dn),
            r_copy(part.at[i, t_up, hi], r2.at[0, i, hi], r2_send.at[0, 1, i], r2_recv.at[0, 1, i], t_up),
            r_copy(part.at[i, t_dn, lo], r2.at[1, i, lo], r2_send.at[1, 0, i], r2_recv.at[1, 0, i], t_dn),
        ]

    def second_copies(i):
        return [
            r_copy(part.at[i, t_up, lo], r2.at[0, i, lo], r2_send.at[0, 0, i], r2_recv.at[0, 0, i], t_up),
            r_copy(part.at[i, t_dn, hi], r2.at[1, i, hi], r2_send.at[1, 1, i], r2_recv.at[1, 1, i], t_dn),
        ]

    def back_copy(i):
        return pltpu.make_async_remote_copy(
            src_ref=red.at[i], dst_ref=ret.at[e, rem(i, 2)], send_sem=ret_send.at[i], recv_sem=ret_recv.at[i],
            device_id={"tp": t, "ep": source_ep(div(i, 2))}, device_id_type=MESH)

    def relay_sums(i):
        first = first_copies(i)
        first[0].wait_recv()
        part[i, t_up, lo, :] = part[i, t_up, lo, :] + r1[0, i]
        second = second_copies(i)
        second[0].start()
        first[1].wait_recv()
        part[i, t_dn, hi, :] = part[i, t_dn, hi, :] + r1[1, i]
        second[1].start()

    def finish(i):
        first = first_copies(i)
        second = second_copies(i)
        first[2].wait_recv()
        first[3].wait_recv()
        second[0].wait_recv()
        second[1].wait_recv()
        total = (part[i, t] + r2[0, i] + r2[1, i]).astype(jnp.bfloat16)

        @pl.when(i < 2)
        def _():
            ret[e, rem(i, 2)] = total

        @pl.when(i >= 2)
        def _():
            red[i] = total
            back_copy(i).start()

    def combine(i):
        k = div(i, 2)
        h = rem(i, 2)

        @pl.when(i >= 2)
        def _():
            back_copy(i).wait_recv()
        d = rem(x + n_chip - div(k, 2), n_chip) * 2 + rem(c + k, 2)
        base = (d * 2 + h) * sub_rows
        slot_i = lax.broadcasted_iota(jnp.int32, (n_tok, sub_rows), 1) + base
        rows_in = ret[d, h]
        add = jnp.zeros((n_tok, hidden), jnp.float32)
        for j in range(n_top):
            onehot = jnp.where(slot_col[:, j:j + 1] == slot_i, 1.0, 0.0).astype(jnp.bfloat16)
            add = add + gates[:, j:j + 1] * jnp.dot(onehot, rows_in, preferred_element_type=jnp.float32)
        acc[...] = acc[...] + add

    for copy in w_copies:
        copy.wait()

    def step(i, carry):
        @pl.when(i == 0)
        def _():
            relay(t)

        @pl.when(i == 1)
        def _():
            relay(t_dn)
            relay(t_up)

        @pl.when(i == 3)
        def _():
            relay(t_far)

        @pl.when(i == 8)
        def _():
            for tp in (t, t_dn, t_up, t_far):
                far_block(tp)

        for k in (1, 3, 5, 7):
            @pl.when(i == 2 * k)
            def _(k=k):
                for tp in range(n_tp):
                    wait_full((source_ep(k), tp))

        @pl.when(i < n_sub)
        def _():
            @pl.when(rem(i, 2) == 0)
            def _():
                pick(source_ep(div(i, 2)))
            ffn(i)
            for copy in first_copies(i):
                copy.start()

        @pl.when((i >= 1) & (i < n_sub + 1))
        def _():
            relay_sums(i - 1)

        @pl.when((i >= 2) & (i < n_sub + 2))
        def _():
            finish(i - 2)

        @pl.when(i >= 3)
        def _():
            combine(i - 3)
        return carry

    lax.fori_loop(0, n_sub + 3, step, 0)
    out[...] = acc[...].astype(out.dtype)

    for make in sends:
        make().wait_send()

    def drain(i, carry):
        for copy in first_copies(i) + second_copies(i):
            copy.wait_send()

        @pl.when(i >= 2)
        def _():
            back_copy(i).wait_send()
        return carry

    lax.fori_loop(0, n_sub, drain, 0)


def solution(mesh):
    n_tp, n_ep = mesh.shape["tp"], mesh.shape["ep"]
    row_spec = P(("dp", "ep", "tp"), None)

    def local_moe(tokens, expert_ids, gate_vals, w_up, w_down):
        n_tok, hidden = tokens.shape
        n_top = expert_ids.shape[1]
        n_loc, _, ffn_dim = w_up.shape
        n_exp = n_loc * n_ep
        slot_cap = capacity(n_tok, n_top, n_exp)
        id_row = jnp.zeros((ID_ROWS, hidden), jnp.bfloat16)
        flat = expert_ids.T.reshape(1, n_top * n_tok).astype(jnp.bfloat16)
        id_row = jnp.pad(flat, ((0, ID_ROWS - 1), (0, hidden - n_top * n_tok)))
        rows = n_tok + ID_ROWS
        n_src = n_ep * n_tp
        n_sub = 2 * n_ep
        sub_rows = n_loc // 2 * slot_cap
        any_spec = pl.BlockSpec(memory_space=pl.ANY)
        vmem_spec = pl.BlockSpec(memory_space=pltpu.VMEM)
        dma = pltpu.SemaphoreType.DMA
        return pl.pallas_call(
            functools.partial(moe_kernel, n_tp, n_ep, slot_cap),
            out_shape=jax.ShapeDtypeStruct((n_tok, hidden), jnp.bfloat16),
            in_specs=[any_spec, any_spec, vmem_spec, vmem_spec, any_spec, any_spec],
            out_specs=vmem_spec,
            scratch_shapes=[
                pltpu.VMEM((n_src, rows, hidden), jnp.bfloat16),
                pltpu.VMEM((n_loc, hidden, ffn_dim), jnp.bfloat16),
                pltpu.VMEM((n_loc, ffn_dim, hidden), jnp.bfloat16),
                pltpu.VMEM((n_tok, n_tok), jnp.bfloat16),
                pltpu.VMEM((n_loc, n_tp * slot_cap, hidden), jnp.bfloat16),
                pltpu.VMEM((n_sub, n_tp, sub_rows, hidden), jnp.float32),
                pltpu.VMEM((2, n_sub, sub_rows // 2, hidden), jnp.float32),
                pltpu.VMEM((2, n_sub, sub_rows, hidden), jnp.float32),
                pltpu.VMEM((n_sub, sub_rows, hidden), jnp.bfloat16),
                pltpu.VMEM((n_ep, 2, sub_rows, hidden), jnp.bfloat16),
                pltpu.VMEM((n_tok, n_top), jnp.int32),
                pltpu.VMEM((n_tok, hidden), jnp.float32),
                dma((2,)), dma((2, n_loc)),
                dma((n_src,)), dma((n_src,)), dma((n_src,)), dma((2, n_src)),
                dma((2, n_sub)), dma((2, n_sub)),
                dma((2, 2, n_sub)), dma((2, 2, n_sub)),
                dma((n_sub,)), dma((n_sub,)),
            ],
            compiler_params=pltpu.CompilerParams(
                collective_id=0, has_side_effects=True, vmem_limit_bytes=67043328),
        )(tokens, id_row, expert_ids, gate_vals, w_up, w_down)

    return jax.shard_map(local_moe, mesh=mesh,
                         in_specs=(row_spec, row_spec, row_spec, P("ep", None, "tp"), P("ep", "tp", None)),
                         out_specs=row_spec, check_vma=False)
```

time: 272 us -> 160 us (0.59)
  waiting for transfers between devices: 198 us -> 0 us
  Pallas kernels: 0 us -> 154 us
  blocking collectives: 26.4 us -> 0 us
  matrix products: 20.2 us -> 0 us
  between operations: 13.5 us -> 0.01 us
  starting transfers between devices: 5.26 us -> 0 us
  other arithmetic: 4.95 us -> 0.68 us
    pallas_call x0 -> x1, Pallas kernels: none -> 154 us  [local_moe(): pl.pallas_call(functools.partial(moe_kernel, n_tp, n_ep, slot_cap), out_s...]
    reduce_scatter x1 -> x0, waiting for transfers between devices: 113 us -> none  [local_moe(): lax.psum_scatter(part_out, 'tp', scatter_dimension=1, tiled=True)]
    all_gather x1 -> x0, waiting for transfers between devices: 64.5 us -> none  [local_moe(): gathered = lax.all_gather(arrived, 'tp', axis=1, tiled=True)]
    all_to_all x1 -> x0, blocking collectives: 26.4 us -> none  [local_moe(): arrived = lax.all_to_all(send_buf, 'ep', 0, 1, tiled=True)]
    all_to_all x1 -> x0, waiting for transfers between devices: 20.4 us -> none  [local_moe(): lax.all_to_all(reduced, 'ep', 1, 0, tiled=True).reshape(n_slots, hidden)]
    dot_general x4 -> x0, matrix products: 20.2 us -> none  [the longest x1 17.5 us: local_moe(): jnp.einsum('ecf,efh->ech', hidden_act, w_down, preferred_element_type=jnp...]
    all_to_all x1 -> x0, starting transfers between devices: 5.19 us -> none  [local_moe(): lax.all_to_all(reduced, 'ep', 1, 0, tiled=True).reshape(n_slots, hidden)]
    unnamed x4, local copies, waits for them, and re-layouts: 0.01 us -> 4.72 us
  transfers between devices with their start and end apart: 3 -> 0, of which waited for: 3 -> 0; matrix products, arithmetic and copies ran while one was open for 0% -> 0% of each run, Pallas kernels for 0% -> 0%
where the time goes in v1:
time: 160 us
  Pallas kernels  154 us (96%)
  local copies, waits for them, and re-layouts  5.32 us (3%)
    pallas_call x1, Pallas kernels, local_moe(): pl.pallas_call(functools.partial(moe_kernel, n_tp, n_ep, slot_cap), out_s...  154 us
    unnamed x4, local copies, waits for them, and re-layouts  4.72 us

profile of v1, /device:TPU:97, one launch (start us, length us, event | category | flops | bytes accessed | tf_op | source)
XLA Modules:
  0.0 160.1 jit_solution(9545152364664004176)
XLA Ops:
  0.0 0.7 convert_bitcast_fusion
  0.7 0.6 pad.4.id_rows
  1.3 1.5 copy.7.gates
  2.8 1.5 copy.6.ids_col
  4.2 154.0 %shard_map.55 = bf16[256,768]{1,0:T(8,128)(2,1)} custom-call(bf16[256,768]{1,0:T(8,128)(2,1)} %tokens.1, bf16[16,768]{1,0:T(8,128)(2,1)} %pad.4.id_rows, s32[256,2]{1,0:T(8,128)} %copy.6.ids_col, f32[256,2]{1,0:T(8,128)} %copy.7.gates, bf16[8,768,768]{2,1,0:T(8,128)(2,1)} %w_up.1, bf16[8,768,768]{2,1,0:T(8,128)(2,1)} %w_down.1), custom_call_target="tpu_custom_call" | custom-call | tf_op jit(solution)/shard_map/pallas_call | solution.py:376
  158.3 1.8 %copy.10 = bf16[256,768]{1,0:T(8,128)(2,1)} copy(bf16[256,768]{1,0:T(8,128)(2,1)} %shard_map.55) | data formatting | bytes 786432
  (1 shorter events, 0.0 us)

commit v2 on v1

--- a/solution.py
+++ b/solution.py
@@ -23,8 +23,8 @@
     return a // b if isinstance(a, int) else lax.div(a, b)
 
 
-def moe_kernel(n_tp, n_ep, slot_cap, tokens, id_rows, ids_col, gates, w_up, w_down, out,
-               tok, up, down, tri, xbuf, part, r1, r2, red, ret, slot_col, acc,
+def moe_kernel(n_tp, n_ep, slot_cap, tokens, ids_row, gates_row, w_up, w_down, out,
+               tok, up, down, tri, xbuf, part, r1, r2, red, ret, slot_col, gates, acc,
                load_sem, w_sem, full_send, full_recv, half_send, half_recv,
                r1_send, r1_recv, r2_send, r2_recv, ret_send, ret_recv):
     t = lax.axis_index("tp")
@@ -34,7 +34,7 @@
     c = rem(e, 2)
     n_tok, hidden = tokens.shape
     n_loc = w_up.shape[0]
-    n_top = ids_col.shape[1]
+    n_top = ids_row.shape[0]
     n_exp = n_loc * n_ep
     rows = n_tok + ID_ROWS
     half_rows = n_tok // 2
@@ -56,12 +56,8 @@
         return ep * n_tp + tp
 
     own = block(e, t)
-    own_copies = [
-        pltpu.make_async_copy(tokens, tok.at[own, pl.ds(0, n_tok)], load_sem.at[0]),
-        pltpu.make_async_copy(id_rows, tok.at[own, pl.ds(n_tok, ID_ROWS)], load_sem.at[1]),
-    ]
-    for copy in own_copies:
-        copy.start()
+    own_copy = pltpu.make_async_copy(tokens, tok.at[own, pl.ds(0, n_tok)], load_sem)
+    own_copy.start()
     w_copies = []
     for i in range(n_loc):
         w_copies.append(pltpu.make_async_copy(w_up.at[i], up.at[i], w_sem.at[0, i]))
@@ -74,6 +70,15 @@
         pl.semaphore_signal(barrier, inc=1, device_id={"tp": tp, "ep": e}, device_id_type=MESH)
     for step in range(1, n_ep):
         pl.semaphore_signal(barrier, inc=1, device_id={"tp": t, "ep": rem(e + step, n_ep)}, device_id_type=MESH)
+
+    ids_f = ids_row[...].astype(jnp.float32)
+    flat = [ids_f[j:j + 1] for j in range(n_top)] + [jnp.zeros((1, hidden - n_top * n_tok), jnp.float32)]
+    flat = jnp.concatenate(flat, axis=1).astype(jnp.bfloat16)
+    tok[own, n_tok:rows, :] = jnp.broadcast_to(flat, (ID_ROWS, hidden))
+    both = jnp.concatenate([ids_f, gates_row[...], jnp.zeros((8 - 2 * n_top, n_tok), jnp.float32)], axis=0)
+    both = jnp.transpose(both)
+    gates[...] = both[:, n_top:2 * n_top]
+    ids_col = both[:, 0:n_top].astype(jnp.int32)
 
     row_i = lax.broadcasted_iota(jnp.int32, (n_tok, n_tok), 0)
     col_i = lax.broadcasted_iota(jnp.int32, (n_tok, n_tok), 1)
@@ -140,8 +145,7 @@
         send_full(src, t, dn_ep)
         send_full(src, t, mate_ep)
 
-    for copy in own_copies:
-        copy.wait()
+    own_copy.wait()
     pl.semaphore_wait(barrier, n_ep + 1)
     send_full((e, t), t_up, e)
     send_full((e, t), t_dn, e)
@@ -298,7 +302,7 @@
             relay(t_dn)
             relay(t_up)
 
-        @pl.when(i == 3)
+        @pl.when(i == 4)
         def _():
             relay(t_far)
 
@@ -326,16 +330,16 @@
         def _():
             relay_sums(i - 1)
 
-        @pl.when((i >= 2) & (i < n_sub + 2))
-        def _():
-            finish(i - 2)
-
-        @pl.when(i >= 3)
-        def _():
-            combine(i - 3)
+        @pl.when((i >= 3) & (i < n_sub + 3))
+        def _():
+            finish(i - 3)
+
+        @pl.when(i >= 5)
+        def _():
+            combine(i - 5)
         return carry
 
-    lax.fori_loop(0, n_sub + 3, step, 0)
+    lax.fori_loop(0, n_sub + 5, step, 0)
     out[...] = acc[...].astype(out.dtype)
 
     for make in sends:
@@ -363,9 +367,6 @@
         n_loc, _, ffn_dim = w_up.shape
         n_exp = n_loc * n_ep
         slot_cap = capacity(n_tok, n_top, n_exp)
-        id_row = jnp.zeros((ID_ROWS, hidden), jnp.bfloat16)
-        flat = expert_ids.T.reshape(1, n_top * n_tok).astype(jnp.bfloat16)
-        id_row = jnp.pad(flat, ((0, ID_ROWS - 1), (0, hidden - n_top * n_tok)))
         rows = n_tok + ID_ROWS
         n_src = n_ep * n_tp
         n_sub = 2 * n_ep
@@ -376,7 +377,7 @@
         return pl.pallas_call(
             functools.partial(moe_kernel, n_tp, n_ep, slot_cap),
             out_shape=jax.ShapeDtypeStruct((n_tok, hidden), jnp.bfloat16),
-            in_specs=[any_spec, any_spec, vmem_spec, vmem_spec, any_spec, any_spec],
+            in_specs=[any_spec, vmem_spec, vmem_spec, any_spec, any_spec],
             out_specs=vmem_spec,
             scratch_shapes=[
                 pltpu.VMEM((n_src, rows, hidden), jnp.bfloat16),
@@ -390,8 +391,9 @@
                 pltpu.VMEM((n_sub, sub_rows, hidden), jnp.bfloat16),
                 pltpu.VMEM((n_ep, 2, sub_rows, hidden), jnp.bfloat16),
                 pltpu.VMEM((n_tok, n_top), jnp.int32),
+                pltpu.VMEM((n_tok, n_top), jnp.float32),
                 pltpu.VMEM((n_tok, hidden), jnp.float32),
-                dma((2,)), dma((2, n_loc)),
+                dma, dma((2, n_loc)),
                 dma((n_src,)), dma((n_src,)), dma((n_src,)), dma((2, n_src)),
                 dma((2, n_sub)), dma((2, n_sub)),
                 dma((2, 2, n_sub)), dma((2, 2, n_sub)),
@@ -399,7 +401,7 @@
             ],
             compiler_params=pltpu.CompilerParams(
                 collective_id=0, has_side_effects=True, vmem_limit_bytes=67043328),
-        )(tokens, id_row, expert_ids, gate_vals, w_up, w_down)
+        )(tokens, expert_ids.T, gate_vals.T, w_up, w_down)
 
     return jax.shard_map(local_moe, mesh=mesh,
                          in_specs=(row_spec, row_spec, row_spec, P("ep", None, "tp"), P("ep", "tp", None)),

time: 160 us -> 154 us (0.963)
  local copies, waits for them, and re-layouts: 5.32 us -> 1.77 us
  Pallas kernels: 154 us -> 152 us
    unnamed x4 -> x1, local copies, waits for them, and re-layouts: 4.72 us -> 1.77 us
    pallas_call x1, Pallas kernels: 154 us -> 152 us  [local_moe(): pl.pallas_call(functools.partial(moe_kernel, n_tp, n_ep, slot_cap), out_s...]
where the time goes in v2:
time: 154 us; the launch traced here: 153 us
  Pallas kernels  152 us (99%)
  local copies, waits for them, and re-layouts  1.77 us (1%)
    pallas_call x1, Pallas kernels, local_moe(): pl.pallas_call(functools.partial(moe_kernel, n_tp, n_ep, slot_cap), out_s...  152 us

profile of v2, /device:TPU:97, one launch (start us, length us, event | category | flops | bytes accessed | tf_op | source)
XLA Modules:
  0.0 153.4 jit_solution(10960413580273632951)
XLA Ops:
  0.0 151.6 %shard_map.55 = bf16[256,768]{1,0:T(8,128)(2,1)} custom-call(bf16[256,768]{1,0:T(8,128)(2,1)} %tokens.1, s32[2,256]{1,0:T(2,128)} %bitcast.2, f32[2,256]{1,0:T(2,128)} %bitcast.3, bf16[8,768,768]{2,1,0:T(8,128)(2,1)} %w_up.1, bf16[8,768,768]{2,1,0:T(8,128)(2,1)} %w_down.1), custom_call_target="tpu_custom_call" | custom-call | tf_op jit(solution)/shard_map/pallas_call | solution.py:377
  151.7 1.8 %copy.7 = bf16[256,768]{1,0:T(8,128)(2,1)} copy(bf16[256,768]{1,0:T(8,128)(2,1)} %shard_map.55) | data formatting | bytes 786432
